TPU v7x, 32 devices: a whole 2x2x4 slice. The times are simulated.
32 devices in a mesh: expert: 16 (over z, y, x), shard: 2 (over core).
Axes of the slice: x: 2, y: 2, z: 4, core: 2. Of those that a mesh axis runs over, the one named last changes fastest.
Arguments:
- w_gate: float32 [64, 2048, 1024], P('expert', 'shard'), may hold values from -0.125 to 0.125
- avg_gate: float32 [64, 2048, 1024], P('expert', 'shard'), may hold values from -0.125 to 0.125
- w_up: float32 [64, 2048, 1024], P('expert', 'shard'), may hold values from -0.125 to 0.125
- avg_up: float32 [64, 2048, 1024], P('expert', 'shard'), may hold values from -0.125 to 0.125
- mix_share: float32 [64], P('expert'), may hold values from 0.2 to 0.8
- router_weight: float32 [2048, 64], P('shard', 'expert'), may hold values from -0.125 to 0.125
- router_gain: float32 [2048], P('shard'), may hold values from 0.25 to 1.75
Outputs:
- serve_gate: bfloat16 [64, 1024, 2048], P('expert')
- serve_up: bfloat16 [64, 1024, 2048], P('expert')
- serve_router: bfloat16 [2048, 64], replicated
All inputs are finite; a program needn't handle non-finite values.
Results may differ from a plain program's by a relative error of at most 0.001.
Values may be sent and summed in bfloat16 or wider, within the bound.
A program may use at most 192 MiB of HBM per device.

v0:
```python
import jax
import jax.numpy as jnp
from jax import lax
from jax.sharding import PartitionSpec as P


def local(w_gate, avg_gate, w_up, avg_up, mix_share, router_weight, router_gain):
    fresh_gate = mix_share[:, None, None] * w_gate + (1.0 - mix_share[:, None, None]) * avg_gate
    fresh_up = mix_share[:, None, None] * w_up + (1.0 - mix_share[:, None, None]) * avg_up
    narrow_gate, narrow_up = (fresh_gate.astype(jnp.bfloat16), fresh_up.astype(jnp.bfloat16))
    serve_gate, serve_up = (
        lax.all_gather(narrow_gate, "shard", axis=1, tiled=True),
        lax.all_gather(narrow_up, "shard", axis=1, tiled=True),
    )
    serve_gate = jnp.transpose(serve_gate, (0, 2, 1))
    serve_up = jnp.transpose(serve_up, (0, 2, 1))
    part_router = (router_weight * router_gain[:, None]).astype(jnp.bfloat16)
    row_router = lax.all_gather(part_router, "shard", axis=0, tiled=True)
    serve_router = lax.all_gather(row_router, "expert", axis=1, tiled=True)
    return (serve_gate, serve_up, serve_router)


def solution(mesh):
    return jax.shard_map(
        local,
        mesh=mesh,
        in_specs=(
            P("expert", "shard", None),
            P("expert", "shard", None),
            P("expert", "shard", None),
            P("expert", "shard", None),
            P("expert"),
            P("shard", "expert"),
            P("shard"),
        ),
        out_specs=(P("expert", None, None), P("expert", None, None), P()),
        check_vma=False,
    )
```

profile of v0, /device:TPU:0, one launch (start us, length us, event | category | flops | bytes accessed | tf_op | source)
XLA Modules:
  0.0 197.7 jit_solution(756094259568171087)
XLA Ops:
  7.2 0.0 all-gather.4.cloned.1.call-start
  7.2 16.4 %copy.14 = f32[4,1024,1024]{1,2,0:T(8,128)} copy(f32[4,1024,1024]{2,1,0:T(8,128)} %param.7) | data formatting | bytes 33554432 | tf_op args[0]
  23.6 16.4 %copy.15 = f32[4,1024,1024]{1,2,0:T(8,128)} copy(f32[4,1024,1024]{2,1,0:T(8,128)} %param.8) | data formatting | bytes 33554432 | tf_op args[1]
  40.0 16.4 %copy.16 = f32[4,1024,1024]{1,2,0:T(8,128)} copy(f32[4,1024,1024]{2,1,0:T(8,128)} %param.9) | data formatting | bytes 33554432 | tf_op args[2]
  56.4 0.0 copy-start.3
  56.4 16.4 %copy.17 = f32[4,1024,1024]{1,2,0:T(8,128)} copy(f32[4,1024,1024]{2,1,0:T(8,128)} %param.10) | data formatting | bytes 33554432 | tf_op args[3]
  72.8 0.0 copy-done.3
  72.8 29.3 %add_convert_fusion = (bf16[4,1024,1024]{1,2,0:T(8,128)(2,1)}, bf16[4,1024,1024]{1,2,0:T(8,128)(2,1)}) fusion(f32[4,1024,1024]{1,2,0:T(8,128)} %copy.17, f32[4,1024,1024]{1,2,0:T(8,128)} %copy.16, f32[4]{0:T(128)S(1)} %broadcast_subtract_fusion, f32[4]{0:T(128)S(1)} %copy-done.3, f32[4,1024,1024]{1,2,0:T(8,128)} %copy.15, f32[4,1024,1024]{1,2,0:T(8,128)} %copy.14), kind=kLoop, calls=%fused_computation | loop fusion | flops 33554432 | bytes 83886112 | tf_op jit(solution)/shard_map/convert_element_type | solution.py:10
  102.0 0.0 copy-start.1
  102.0 0.0 copy-start.2
  102.1 0.0 all-gather.4.cloned.1.call-update
  102.1 0.0 all-gather.6.cloned.1.call-start
  102.1 0.7 all-gather.6.cloned.1.call-update
  102.8 0.0 copy-done.1
  102.8 0.0 copy-done.2
  102.9 2.0 all_gather.14
  104.8 43.6 %all-gather = bf16[16,4,2048]{2,1,0:T(4,128)(2,1)S(1)} all-gather(bf16[1,4,2048]{2,1,0:T(4,128)(2,1)S(1)} %bitcast.9), channel_id=1, replica_groups=mesh['expert'=16,'shard'=2] {'expert'}, dimensions={0}, use_global_device_ids=true | all-gather | bytes 278528 | tf_op jit(solution)/shard_map/all_gather | solution.py:19
  148.5 0.8 reshape.11
  149.2 0.0 all-gather.4.cloned.1.call-done
  149.2 18.6 %all-gather.6.cloned.1.call-done = bf16[4,2048,1024]{1,2,0:T(8,128)(2,1)} async-done(((bf16[4,1024,1024]{1,2,0:T(8,128)(2,1)}), bf16[4,2048,1024]{1,2,0:T(8,128)(2,1)}) %all-gather.6.cloned.1.call-update) | async-done | bytes 16777232 | tf_op jit(solution)/shard_map/all_gather | solution.py:13
  167.9 0.0 copy-start
  167.9 15.1 %copy.20 = bf16[4,1024,2048]{2,1,0:T(8,128)(2,1)} copy(bf16[4,1024,2048]{2,1,0:T(8,128)(2,1)} %bitcast.6) | data formatting | bytes 33554432
  182.9 1.8 copy-done
  184.7 6.2 %copy.21 = bf16[4,1024,2048]{2,1,0:T(8,128)(2,1)} copy(bf16[4,1024,2048]{2,1,0:T(8,128)(2,1)S(1)} %bitcast.7) | data formatting | bytes 33554432
  (2 shorter events, 0.0 us)
Async XLA Ops:
  7.2 142.1 %all-gather.4.cloned.1.call-start = ((), (), s32[]{:S(2)}) async-start(), calls=%async_computation | async-start | bytes 25165824 | tf_op jit(solution)/shard_map/all_gather | solution.py:12
  56.4 16.4 %copy-start.3 = (f32[4]{0:T(128)S(1)}, f32[4]{0:T(128)}, u32[]{:S(2)}) copy-start(f32[4]{0:T(128)} %param.11) | copy-start | bytes 52
  102.0 0.8 copy-start.1
  102.0 0.8 copy-start.2
  102.1 65.8 %all-gather.6.cloned.1.call-start = ((), (), s32[]{:S(2)}) async-start(), calls=%async_computation.1 | async-start | bytes 25165824 | tf_op jit(solution)/shard_map/all_gather | solution.py:13
  167.9 16.9 %copy-start = (bf16[4,2048,1024]{1,2,0:T(8,128)(2,1)S(1)}, bf16[4,2048,1024]{1,2,0:T(8,128)(2,1)}, u32[]{:S(2)}) copy-start(bf16[4,2048,1024]{1,2,0:T(8,128)(2,1)} %all-gather.6.cloned.1.call-done) | copy-start | bytes 50331652
Sparse Core Ops, SparseCore 0:
  102.2 32.7 all-gather.3
  136.6 31.2 all-gather.5
where the time goes:
time: 199 us; the launch traced here: 198 us
  local copies, waits for them, and re-layouts  89.4 us (45%)
  blocking collectives  45.6 us (23%)
  other arithmetic  29.3 us (15%)
  waiting for transfers between devices  19.3 us (10%)
  between operations  14.1 us (7%)
    unnamed x15, local copies, waits for them, and re-layouts  89.4 us
    all_gather x1, blocking collectives, local(): serve_router = lax.all_gather(row_router, 'expert', axis=1, tiled=True)  43.6 us
    convert_element_type x1, other arithmetic, local(): fresh_up.astype(jnp.bfloat16)  29.3 us
    all_gather x1, waiting for transfers between devices, local(): lax.all_gather(narrow_up, 'shard', axis=1, tiled=True)  18.6 us
  transfers between devices with their start and end apart: 2, of which 1 were waited for; matrix products, arithmetic and copies ran while one was open for 0% of the time, Pallas kernels for 0%

commit v1 on v0

v1 whole, which is shorter than its diff:
```python
import functools

import jax
import jax.numpy as jnp
from jax import lax
from jax.experimental import pallas as pl
from jax.experimental.pallas import tpu as pltpu
from jax.sharding import PartitionSpec as P

MESH = pl.DeviceIdType.MESH
SLOTS = 4
ROWS = 256


def mix_kernel(peers, shards, rows, with_router, *refs):
    if with_router:
        (w_ref, avg_ref, mix_ref, weight_ref, gain_ref, out_ref, router_ref,
         w_buf, avg_buf, in_sem, send_sem, recv_sem,
         stage, total, hop_send, hop_recv, row_send, row_recv) = refs
    else:
        (w_ref, avg_ref, mix_ref, out_ref,
         w_buf, avg_buf, in_sem, send_sem, recv_sem) = refs
    me, at = lax.axis_index("shard"), lax.axis_index("expert")
    experts, depth, _ = w_ref.shape
    per = depth // rows
    pieces = experts * per

    def load(i):
        slot = lax.rem(i, SLOTS)
        expert, row = lax.div(i, per), pl.multiple_of(lax.rem(i, per) * rows, rows)
        return [
            pltpu.make_async_copy(src.at[expert, pl.ds(row, rows), :], buf.at[slot], in_sem.at[n, slot])
            for n, (src, buf) in enumerate(((w_ref, w_buf), (avg_ref, avg_buf)))
        ]

    def block(i, owner):
        expert = lax.div(i, per)
        column = pl.multiple_of(owner * depth + lax.rem(i, per) * rows, rows)
        return out_ref.at[expert, :, pl.ds(column, rows)]

    def exchange(i, owner, k):
        return pltpu.make_async_remote_copy(
            src_ref=block(i, owner), dst_ref=block(i, owner),
            send_sem=send_sem.at[k - 1, i], recv_sem=recv_sem.at[k - 1, i],
            device_id={"shard": lax.rem(me + k, shards)}, device_id_type=MESH,
        )

    for i in range(min(SLOTS, pieces)):
        for copy in load(i):
            copy.start()

    barrier = pltpu.get_barrier_semaphore()
    for k in range(1, shards):
        pl.semaphore_signal(barrier, inc=1, device_id={"shard": lax.rem(me + k, shards)}, device_id_type=MESH)
    if with_router:
        @pl.loop(1, peers)
        def _(k):
            pl.semaphore_signal(barrier, inc=1, device_id={"expert": lax.rem(at + k, peers)}, device_id_type=MESH)
    pl.semaphore_wait(barrier, shards - 1 + (peers - 1 if with_router else 0))

    if with_router:
        mine = pl.ds(pl.multiple_of(me * depth, depth), depth)
        stage[at, :, mine] = (weight_ref[...] * gain_ref[...]).astype(jnp.bfloat16)

        def hop(k):
            return pltpu.make_async_remote_copy(
                src_ref=stage.at[at, :, mine], dst_ref=stage.at[at, :, mine],
                send_sem=hop_send.at[k - 1], recv_sem=hop_recv.at[k - 1],
                device_id={"expert": lax.rem(at + k, peers)}, device_id_type=MESH,
            )

        def hop_in(k):
            source = lax.rem(at + peers - k, peers)
            return pltpu.make_async_remote_copy(
                src_ref=stage.at[source, :, mine], dst_ref=stage.at[source, :, mine],
                send_sem=hop_send.at[k - 1], recv_sem=hop_recv.at[k - 1],
                device_id={"expert": lax.rem(at + k, peers)}, device_id_type=MESH,
            )

        @pl.loop(1, peers)
        def _(k):
            hop(k).start()

    @pl.loop(0, pieces)
    def _(i):
        slot = lax.rem(i, SLOTS)
        for copy in load(i):
            copy.wait()
        share = mix_ref[lax.div(i, per)]
        fresh = share * w_buf[slot] + (1.0 - share) * avg_buf[slot]
        block(i, me)[...] = jnp.transpose(fresh.astype(jnp.bfloat16))
        for k in range(1, shards):
            exchange(i, me, k).start()

        @pl.when(i + SLOTS < pieces)
        def _():
            for copy in load(i + SLOTS):
                copy.start()

    if with_router:
        @pl.loop(1, peers)
        def _(k):
            hop(k).wait_send()
            hop_in(k).wait_recv()

        def rows_to(owner, k):
            columns = pl.ds(pl.multiple_of(owner * depth, depth), depth)
            return pltpu.make_async_remote_copy(
                src_ref=stage.at[:, :, columns], dst_ref=stage.at[:, :, columns],
                send_sem=row_send.at[k - 1], recv_sem=row_recv.at[k - 1],
                device_id={"shard": lax.rem(me + k, shards)}, device_id_type=MESH,
            )

        for k in range(1, shards):
            rows_to(me, k).start()
        for k in range(1, shards):
            rows_to(me, k).wait_send()
            rows_to(lax.rem(me + shards - k, shards), k).wait_recv()
        held = stage.shape[1]
        for e in range(peers):
            total[e * held:(e + 1) * held, :] = stage[e].astype(jnp.float32)
        router_ref[...] = total[...].astype(jnp.bfloat16)

    @pl.loop(0, pieces)
    def _(i):
        for k in range(1, shards):
            exchange(i, me, k).wait_send()
            exchange(i, lax.rem(me + shards - k, shards), k).wait_recv()


def mix(mesh, w, avg, share, router=None):
    peers, shards = mesh.shape["expert"], mesh.shape["shard"]
    experts, depth, width = w.shape
    rows = min(ROWS, depth)
    pieces = experts * (depth // rows)
    others = max(shards - 1, 1)
    any_spec = pl.BlockSpec(memory_space=pltpu.HBM)
    vmem_spec = pl.BlockSpec(memory_space=pltpu.VMEM)
    out_shape = [pltpu.VMEM((experts, width, shards * depth), jnp.bfloat16)]
    in_specs = [any_spec, any_spec, pl.BlockSpec(memory_space=pltpu.SMEM)]
    scratch = [
        pltpu.VMEM((SLOTS, rows, width), jnp.float32),
        pltpu.VMEM((SLOTS, rows, width), jnp.float32),
        pltpu.SemaphoreType.DMA((2, SLOTS)),
        pltpu.SemaphoreType.DMA((others, pieces)),
        pltpu.SemaphoreType.DMA((others, pieces)),
    ]
    args = tuple(pltpu.with_memory_space_constraint(x, pltpu.HBM) for x in (w, avg)) + (share,)
    if router is not None:
        args += router
        in_specs += [vmem_spec, vmem_spec]
        out_shape += [pltpu.VMEM((peers * experts, shards * depth), jnp.bfloat16)]
        scratch += [
            pltpu.VMEM((peers, experts, shards * depth), jnp.bfloat16),
            pltpu.VMEM((peers * experts, shards * depth), jnp.float32),
            pltpu.SemaphoreType.DMA((peers,)),
            pltpu.SemaphoreType.DMA((peers,)),
            pltpu.SemaphoreType.DMA((others,)),
            pltpu.SemaphoreType.DMA((others,)),
        ]
    return pl.pallas_call(
        functools.partial(mix_kernel, peers, shards, rows, router is not None),
        out_shape=out_shape,
        in_specs=in_specs,
        out_specs=[vmem_spec] * len(out_shape),
        scratch_shapes=scratch,
        compiler_params=pltpu.CompilerParams(
            collective_id=0 if router is not None else 1,
            has_side_effects=True,
            vmem_limit_bytes=20 * 2**20,
        ),
    )(*args)


def solution(mesh):
    def local(w_gate, avg_gate, w_up, avg_up, mix_share, router_weight, router_gain):
        serve_gate, router = mix(
            mesh, w_gate, avg_gate, mix_share, (router_weight.T, router_gain[None, :])
        )
        serve_up, = mix(mesh, w_up, avg_up, mix_share)
        return serve_gate, serve_up, router.T

    return jax.shard_map(
        local,
        mesh=mesh,
        in_specs=(
            P("expert", "shard", None),
            P("expert", "shard", None),
            P("expert", "shard", None),
            P("expert", "shard", None),
            P("expert"),
            P("shard", "expert"),
            P("shard"),
        ),
        out_specs=(P("expert", None, None), P("expert", None, None), P()),
        check_vma=False,
    )
```

time: 199 us -> 51.7 us (0.26)
  local copies, waits for them, and re-layouts: 89.4 us -> 13.7 us
  blocking collectives: 45.6 us -> 0 us
  Pallas kernels: 0 us -> 37.2 us
  other arithmetic: 29.3 us -> 0 us
  waiting for transfers between devices: 19.3 us -> 0 us
  between operations: 14.1 us -> 0.67 us
    unnamed x15 -> x9, local copies, waits for them, and re-layouts: 89.4 us -> 13.7 us
    all_gather x2 -> x0, blocking collectives: 45.6 us -> none  [the longest x1 43.6 us: local(): serve_router = lax.all_gather(row_router, 'expert', axis=1, tiled=True)]
    pallas_call x0 -> x2, Pallas kernels: none -> 37.2 us  [mix(): pl.pallas_call(functools.partial(mix_kernel, peers, shards, rows, router...]
    convert_element_type x2 -> x0, other arithmetic: 29.3 us -> none  [the longest x1 29.3 us: local(): fresh_up.astype(jnp.bfloat16)]
    all_gather x2 -> x0, waiting for transfers between devices: 18.6 us -> none  [the longest x1 18.6 us: local(): lax.all_gather(narrow_up, 'shard', axis=1, tiled=True)]
  transfers between devices with their start and end apart: 2 -> 0, of which waited for: 1 -> 0; matrix products, arithmetic and copies ran while one was open for 0% -> 0% of each run, Pallas kernels for 0% -> 0%
where the time goes in v1:
time: 51.7 us; the launch traced here: 51.5 us
  Pallas kernels  37.2 us (72%)
  local copies, waits for them, and re-layouts  13.7 us (26%)
  between operations  0.67 us (1%)
    pallas_call x2, Pallas kernels, mix(): pl.pallas_call(functools.partial(mix_kernel, peers, shards, rows, router...  37.2 us
    unnamed x9, local copies, waits for them, and re-layouts  13.7 us

profile of v1, /device:TPU:0, one launch (start us, length us, event | category | flops | bytes accessed | tf_op | source)
XLA Modules:
  0.0 51.5 jit_solution(6271419389650755890)
XLA Ops:
  0.6 0.0 copy-start.2
  0.6 0.6 %copy-done.2 = f32[4]{0:T(128)S(1)} copy-done((f32[4]{0:T(128)S(1)}, f32[4]{0:T(128)}, u32[]{:S(2)}) %copy-start.2) | copy-done | bytes 40
  1.3 15.8 %shard_map.95 = bf16[4,1024,2048]{2,1,0:T(8,128)(2,1)S(1)} custom-call(f32[4,1024,1024]{2,1,0:T(8,128)} %refs_0_.3, f32[4,1024,1024]{2,1,0:T(8,128)} %refs_1_.3, f32[4]{0:T(128)S(1)} %copy-done.2), custom_call_target="tpu_custom_call" | custom-call | tf_op jit(solution)/shard_map/pallas_call | solution.py:161
  17.1 0.0 copy-start
  17.1 0.0 copy-start.1
  17.1 6.2 %copy.14 = bf16[4,1024,2048]{2,1,0:T(8,128)(2,1)} copy(bf16[4,1024,2048]{2,1,0:T(8,128)(2,1)S(1)} %shard_map.95) | data formatting | bytes 33554432
  23.3 0.0 copy-done
  23.3 0.0 copy-done.1
  23.3 21.4 %shard_map.94 = (bf16[4,1024,2048]{2,1,0:T(8,128)(2,1)S(1)}, bf16[64,2048]{1,0:T(8,128)(2,1)S(1)}) custom-call(f32[4,1024,1024]{2,1,0:T(8,128)} %refs_0_.2, f32[4,1024,1024]{2,1,0:T(8,128)} %refs_1_.2, f32[4]{0:T(128)S(1)} %copy-done.2, f32[4,1024]{1,0:T(4,128)S(1)} %bitcast.4, f32[1,1024]{1,0:T(1,128)S(1)} %bitcast.5), custom_call_target="tpu_custom_call" | custom-call | tf_op jit(solution)/shard_map/pallas_call | solution.py:161
  44.7 6.2 %copy.13 = bf16[4,1024,2048]{2,1,0:T(8,128)(2,1)} copy(bf16[4,1024,2048]{2,1,0:T(8,128)(2,1)S(1)} %get-tuple-element.7) | data formatting | bytes 33554432
  50.8 0.7 %copy.15 = bf16[2048,64]{0,1:T(8,128)(2,1)} copy(bf16[2048,64]{0,1:T(8,128)(2,1)S(1)} %bitcast.3) | data formatting | bytes 524288
Async XLA Ops:
  0.6 0.7 %copy-start.2 = (f32[4]{0:T(128)S(1)}, f32[4]{0:T(128)}, u32[]{:S(2)}) copy-start(f32[4]{0:T(128)} %refs_2_.3) | copy-start | bytes 52
  17.1 6.2 %copy-start = (f32[1024,4]{0,1:T(4,128)S(1)}, f32[1024,4]{0,1:T(4,128)}, u32[]{:S(2)}) copy-start(f32[1024,4]{0,1:T(4,128)} %param.12) | copy-start | bytes 49156
  17.1 6.2 %copy-start.1 = (f32[1024]{0:T(1024)S(1)}, f32[1024]{0:T(1024)}, u32[]{:S(2)}) copy-start(f32[1024]{0:T(1024)} %param.13) | copy-start | bytes 12292

commit v2 on v1

v2 whole, which is shorter than its diff:
```python
import functools

import jax
import jax.numpy as jnp
from jax import lax
from jax.experimental import pallas as pl
from jax.experimental.pallas import tpu as pltpu
from jax.sharding import PartitionSpec as P

MESH = pl.DeviceIdType.MESH
SLOTS = 4
SIZE = 256
BY_COLUMN = True
CUTS = 8


def mix_kernel(peers, shards, size, *refs):
    (w_gate, avg_gate, w_up, avg_up, mix_ref, weight_ref, gain_ref,
     gate_ref, up_ref, router_ref,
     w_buf, avg_buf, in_sem, send_sem, recv_sem,
     stage, total, hop_send, hop_recv, row_send, row_recv) = refs
    me, at = lax.axis_index("shard"), lax.axis_index("expert")
    experts, depth, width = w_gate.shape
    per = (width if BY_COLUMN else depth) // size
    pieces = experts * per
    sources, outs = ((w_gate, avg_gate), (w_up, avg_up)), (gate_ref, up_ref)

    def load(m, i):
        slot = lax.rem(i, SLOTS)
        expert, start = lax.div(i, per), pl.multiple_of(lax.rem(i, per) * size, size)
        def part(src):
            return src.at[expert, :, pl.ds(start, size)] if BY_COLUMN else src.at[expert, pl.ds(start, size), :]
        return [
            pltpu.make_async_copy(part(src), buf.at[slot], in_sem.at[n, slot])
            for n, (src, buf) in enumerate(zip(sources[m], (w_buf, avg_buf)))
        ]

    def block(m, i, owner):
        expert, start = lax.div(i, per), lax.rem(i, per) * size
        if BY_COLUMN:
            column = pl.multiple_of(owner * depth, depth)
            return outs[m].at[expert, pl.ds(pl.multiple_of(start, size), size), pl.ds(column, depth)]
        return outs[m].at[expert, :, pl.ds(pl.multiple_of(owner * depth + start, size), size)]

    def exchange(m, i, owner, k):
        return pltpu.make_async_remote_copy(
            src_ref=block(m, i, owner), dst_ref=block(m, i, owner),
            send_sem=send_sem.at[m, k - 1, i], recv_sem=recv_sem.at[m, k - 1, i],
            device_id={"shard": lax.rem(me + k, shards)}, device_id_type=MESH,
        )

    for i in range(min(SLOTS, pieces)):
        for copy in load(0, i):
            copy.start()

    barrier = pltpu.get_barrier_semaphore()
    for k in range(1, shards):
        pl.semaphore_signal(barrier, inc=1, device_id={"shard": lax.rem(me + k, shards)}, device_id_type=MESH)
    if True:
        @pl.loop(1, peers)
        def _(k):
            pl.semaphore_signal(barrier, inc=1, device_id={"expert": lax.rem(at + k, peers)}, device_id_type=MESH)
    pl.semaphore_wait(barrier, shards - 1 + peers - 1)

    if True:
        mine = pl.ds(pl.multiple_of(me * depth, depth), depth)
        stage[at, :, mine] = (weight_ref[...] * gain_ref[...]).astype(jnp.bfloat16)

        def hop(k):
            return pltpu.make_async_remote_copy(
                src_ref=stage.at[at, :, mine], dst_ref=stage.at[at, :, mine],
                send_sem=hop_send.at[k - 1], recv_sem=hop_recv.at[k - 1],
                device_id={"expert": lax.rem(at + k, peers)}, device_id_type=MESH,
            )

        def hop_in(k):
            source = lax.rem(at + peers - k, peers)
            return pltpu.make_async_remote_copy(
                src_ref=stage.at[source, :, mine], dst_ref=stage.at[source, :, mine],
                send_sem=hop_send.at[k - 1], recv_sem=hop_recv.at[k - 1],
                device_id={"expert": lax.rem(at + k, peers)}, device_id_type=MESH,
            )

        @pl.loop(1, peers)
        def _(k):
            hop(k).start()

    for m in range(2):
        @pl.loop(0, pieces)
        def _(i):
            slot = lax.rem(i, SLOTS)
            for copy in load(m, i):
                copy.wait()
            share = mix_ref[lax.div(i, per)]
            fresh = share * w_buf[slot] + (1.0 - share) * avg_buf[slot]
            block(m, i, me)[...] = jnp.transpose(fresh.astype(jnp.bfloat16))
            for k in range(1, shards):
                exchange(m, i, me, k).start()

            @pl.when(i + SLOTS < pieces)
            def _():
                for copy in load(m, i + SLOTS):
                    copy.start()

            if m == 0:
                @pl.when(i + SLOTS >= pieces)
                def _():
                    for copy in load(1, i + SLOTS - pieces):
                        copy.start()

    if True:
        @pl.loop(1, peers)
        def _(k):
            hop(k).wait_send()
            hop_in(k).wait_recv()

        def rows_to(owner, k):
            columns = pl.ds(pl.multiple_of(owner * depth, depth), depth)
            return pltpu.make_async_remote_copy(
                src_ref=stage.at[:, :, columns], dst_ref=stage.at[:, :, columns],
                send_sem=row_send.at[k - 1], recv_sem=row_recv.at[k - 1],
                device_id={"shard": lax.rem(me + k, shards)}, device_id_type=MESH,
            )

        for k in range(1, shards):
            rows_to(me, k).start()
        for k in range(1, shards):
            rows_to(me, k).wait_send()
            rows_to(lax.rem(me + shards - k, shards), k).wait_recv()
        held = stage.shape[1]
        for e in range(peers):
            total[e * held:(e + 1) * held, :] = stage[e].astype(jnp.float32)
        router_ref[...] = total[...].astype(jnp.bfloat16)

    for m in range(2):
        @pl.loop(0, pieces)
        def _(i):
            for k in range(1, shards):
                exchange(m, i, me, k).wait_send()
                exchange(m, i, lax.rem(me + shards - k, shards), k).wait_recv()


def mix(mesh, sources, share, weight, gain):
    peers, shards = mesh.shape["expert"], mesh.shape["shard"]
    experts, depth, width = sources[0].shape
    span = width if BY_COLUMN else depth
    size = min(SIZE, span)
    pieces = experts * (span // size)
    assert pieces % SLOTS == 0
    others = max(shards - 1, 1)
    hbm_spec = pl.BlockSpec(memory_space=pltpu.HBM)
    vmem_spec = pl.BlockSpec(memory_space=pltpu.VMEM)
    buffer = pltpu.VMEM((SLOTS, depth, size) if BY_COLUMN else (SLOTS, size, width), jnp.float32)
    half = pltpu.VMEM((experts, width, shards * depth), jnp.bfloat16)
    return pl.pallas_call(
        functools.partial(mix_kernel, peers, shards, size),
        out_shape=[half, half, pltpu.VMEM((peers * experts, shards * depth), jnp.bfloat16)],
        in_specs=[hbm_spec] * 4 + [pl.BlockSpec(memory_space=pltpu.SMEM), vmem_spec, vmem_spec],
        out_specs=[vmem_spec] * 3,
        scratch_shapes=[
            buffer,
            buffer,
            pltpu.SemaphoreType.DMA((2, SLOTS)),
            pltpu.SemaphoreType.DMA((2, others, pieces)),
            pltpu.SemaphoreType.DMA((2, others, pieces)),
            pltpu.VMEM((peers, experts, shards * depth), jnp.bfloat16),
            pltpu.VMEM((peers * experts, shards * depth), jnp.float32),
            pltpu.SemaphoreType.DMA((peers,)),
            pltpu.SemaphoreType.DMA((peers,)),
            pltpu.SemaphoreType.DMA((others,)),
            pltpu.SemaphoreType.DMA((others,)),
        ],
        compiler_params=pltpu.CompilerParams(
            collective_id=0, has_side_effects=True, vmem_limit_bytes=12 * 2**20
        ),
    )(*(pltpu.with_memory_space_constraint(x, pltpu.HBM) for x in sources), share, weight, gain)


def store_kernel(*refs):
    count = (len(refs) - 1) // 2
    copies = []
    for n in range(count):
        source, target = refs[n], refs[count + n]
        step = max(source.shape[0] // CUTS, 1) if len(source.shape) == 2 else source.shape[0]
        if len(source.shape) == 3:
            step = source.shape[1] // 2
            for e in range(source.shape[0]):
                for r in range(2):
                    copies.append((source.at[e, pl.ds(r * step, step), :], target.at[e, pl.ds(r * step, step), :]))
        else:
            copies.append((source, target))
    started = [pltpu.make_async_copy(a, b, refs[-1].at[n]) for n, (a, b) in enumerate(copies)]
    for copy in started:
        copy.start()
    for copy in started:
        copy.wait()


def store(*arrays):
    vmem_spec = pl.BlockSpec(memory_space=pltpu.VMEM)
    count = sum(2 * x.shape[0] if x.ndim == 3 else 1 for x in arrays)
    return pl.pallas_call(
        store_kernel,
        out_shape=[pltpu.HBM(x.shape, x.dtype) for x in arrays],
        in_specs=[vmem_spec] * len(arrays),
        out_specs=[pl.BlockSpec(memory_space=pltpu.HBM)] * len(arrays),
        scratch_shapes=[pltpu.SemaphoreType.DMA((count,))],
        compiler_params=pltpu.CompilerParams(vmem_limit_bytes=2**20),
    )(*arrays)


def solution(mesh):
    def local(w_gate, avg_gate, w_up, avg_up, mix_share, router_weight, router_gain):
        gate, up, router = mix(
            mesh, (w_gate, avg_gate, w_up, avg_up), mix_share, router_weight.T, router_gain[None, :]
        )
        gate, up, router = store(gate, up, router)
        return gate, up, router.T

    return jax.shard_map(
        local,
        mesh=mesh,
        in_specs=(
            P("expert", "shard", None),
            P("expert", "shard", None),
            P("expert", "shard", None),
            P("expert", "shard", None),
            P("expert"),
            P("shard", "expert"),
            P("shard"),
        ),
        out_specs=(P("expert", None, None), P("expert", None, None), P()),
        check_vma=False,
    )
```

time: 51.7 us -> 48.2 us (0.932)
  local copies, waits for them, and re-layouts: 13.7 us -> 2.05 us
  Pallas kernels: 37.2 us -> 45.2 us
    unnamed x9 -> x6, local copies, waits for them, and re-layouts: 13.7 us -> 2.05 us
    pallas_call x2, Pallas kernels: 37.2 us -> 45.2 us  [the longest x1 34.2 us: mix(): pl.pallas_call(functools.partial(mix_kernel, peers, shards, size), out_sh...]
where the time goes in v2:
time: 48.2 us; the launch traced here: 47.9 us
  Pallas kernels  45.2 us (94%)
  local copies, waits for them, and re-layouts  2.05 us (4%)
  between operations  0.65 us (1%)
    pallas_call x1, Pallas kernels, mix(): pl.pallas_call(functools.partial(mix_kernel, peers, shards, size), out_sh...  34.2 us
    pallas_call x1, Pallas kernels, store(): pl.pallas_call(store_kernel, out_shape=[pltpu.HBM(x.shape, x.dtype) for x...  11.1 us
    unnamed x6, local copies, waits for them, and re-layouts  2.05 us

profile of v2, /device:TPU:0, one launch (start us, length us, event | category | flops | bytes accessed | tf_op | source)
XLA Modules:
  0.0 47.9 jit_solution(14652578368287349811)
XLA Ops:
  0.6 0.0 copy-start
  0.6 0.7 %copy-done = f32[1024,4]{0,1:T(4,128)S(1)} copy-done((f32[1024,4]{0,1:T(4,128)S(1)}, f32[1024,4]{0,1:T(4,128)}, u32[]{:S(2)}) %copy-start) | copy-done | bytes 16408
  1.4 0.0 copy-start.1
  1.4 0.7 %copy-done.1 = f32[1024]{0:T(1024)S(1)} copy-done((f32[1024]{0:T(1024)S(1)}, f32[1024]{0:T(1024)}, u32[]{:S(2)}) %copy-start.1) | copy-done | bytes 4120
  2.0 0.0 copy-start.2
  2.0 0.7 %copy-done.2 = f32[4]{0:T(128)S(1)} copy-done((f32[4]{0:T(128)S(1)}, f32[4]{0:T(128)}, u32[]{:S(2)}) %copy-start.2) | copy-done | bytes 40
  2.7 34.2 %shard_map.94 = (bf16[4,1024,2048]{2,1,0:T(8,128)(2,1)S(1)}, bf16[4,1024,2048]{2,1,0:T(8,128)(2,1)S(1)}, bf16[64,2048]{1,0:T(8,128)(2,1)S(1)}) custom-call(f32[4,1024,1024]{2,1,0:T(8,128)} %refs_0_.1, f32[4,1024,1024]{2,1,0:T(8,128)} %refs_1_.1, f32[4,1024,1024]{2,1,0:T(8,128)} %refs_2_.1, f32[4,1024,1024]{2,1,0:T(8,128)} %refs_3_.1, f32[4]{0:T(128)S(1)} %copy-done.2, ...), custom_call_target="tpu_custom_call" | custom-call | tf_op jit(solution)/shard_map/pallas_call | solution.py:155
  36.9 11.1 %shard_map.95 = (bf16[4,1024,2048]{2,1,0:T(8,128)(2,1)}, bf16[4,1024,2048]{2,1,0:T(8,128)(2,1)}, bf16[64,2048]{1,0:T(8,128)(2,1)}) custom-call(bf16[4,1024,2048]{2,1,0:T(8,128)(2,1)S(1)} %get-tuple-element.9.refs_0_, bf16[4,1024,2048]{2,1,0:T(8,128)(2,1)S(1)} %get-tuple-element.10.refs_1_, bf16[64,2048]{1,0:T(8,128)(2,1)S(1)} %get-tuple-element.11.refs_2_), custom_call_target="tpu_custom_call" | custom-call | tf_op jit(solution)/shard_map/pallas_call | solution.py:202
Async XLA Ops:
  0.6 0.7 %copy-start = (f32[1024,4]{0,1:T(4,128)S(1)}, f32[1024,4]{0,1:T(4,128)}, u32[]{:S(2)}) copy-start(f32[1024,4]{0,1:T(4,128)} %param.12) | copy-start | bytes 49156
  1.4 0.7 %copy-start.1 = (f32[1024]{0:T(1024)S(1)}, f32[1024]{0:T(1024)}, u32[]{:S(2)}) copy-start(f32[1024]{0:T(1024)} %param.13) | copy-start | bytes 12292
  2.0 0.7 %copy-start.2 = (f32[4]{0:T(128)S(1)}, f32[4]{0:T(128)}, u32[]{:S(2)}) copy-start(f32[4]{0:T(128)} %refs_4_.1) | copy-start | bytes 52

commit v3 on v1

v3 whole, which is shorter than its diff:
```python
import functools

import jax
import jax.numpy as jnp
from jax import lax
from jax.experimental import pallas as pl
from jax.experimental.pallas import tpu as pltpu
from jax.sharding import PartitionSpec as P

MESH = pl.DeviceIdType.MESH
SLOTS = 4
SIZE = 256
BY_COLUMN = True
EARLY = 2


def mix_kernel(peers, shards, size, plan, with_router, *refs):
    refs = list(refs)
    sources = [(refs.pop(0), refs.pop(0)) for _ in plan]
    mix_ref = refs.pop(0)
    if with_router:
        weight_ref, gain_ref = refs.pop(0), refs.pop(0)
    outs = [refs.pop(0) for _ in plan]
    if with_router:
        router_ref = refs.pop(0)
    w_buf, avg_buf, share_buf, in_sem, share_sem, send_sem, recv_sem = refs[:7]
    if with_router:
        weight_buf, gain_buf, stage, total, small_sem, hop_send, hop_recv, row_send, row_recv = refs[7:]
    me, at = lax.axis_index("shard"), lax.axis_index("expert")
    experts, depth, width = sources[0][0].shape
    per = (width if BY_COLUMN else depth) // size
    counts = [(last - first) * per for first, last, _ in plan]

    def load(m, i):
        slot = lax.rem(i, SLOTS)
        expert, start = plan[m][0] + lax.div(i, per), pl.multiple_of(lax.rem(i, per) * size, size)
        def part(src):
            return src.at[expert, :, pl.ds(start, size)] if BY_COLUMN else src.at[expert, pl.ds(start, size), :]
        return [
            pltpu.make_async_copy(part(src), buf.at[slot], in_sem.at[n, slot])
            for n, (src, buf) in enumerate(zip(sources[m], (w_buf, avg_buf)))
        ]

    def block(m, i, owner):
        expert, start = lax.div(i, per), lax.rem(i, per) * size
        base = owner * depth if plan[m][2] else 0
        if BY_COLUMN:
            column = pl.multiple_of(base, depth) if plan[m][2] else 0
            return outs[m].at[expert, pl.ds(pl.multiple_of(start, size), size), pl.ds(column, depth)]
        return outs[m].at[expert, :, pl.ds(pl.multiple_of(base + start, size), size)]

    def exchange(m, i, owner, k):
        at_sem = sum(c for c, p in zip(counts[:m], plan) if p[2]) + i
        return pltpu.make_async_remote_copy(
            src_ref=block(m, i, owner), dst_ref=block(m, i, owner),
            send_sem=send_sem.at[k - 1, at_sem], recv_sem=recv_sem.at[k - 1, at_sem],
            device_id={"shard": lax.rem(me + k, shards)}, device_id_type=MESH,
        )

    for i in range(SLOTS):
        for copy in load(0, i):
            copy.start()
    if experts > 1:
        share_copy = pltpu.make_async_copy(mix_ref, share_buf, share_sem)
        share_copy.start()
    if with_router:
        small = [
            pltpu.make_async_copy(weight_ref, weight_buf, small_sem.at[0]),
            pltpu.make_async_copy(gain_ref, gain_buf, small_sem.at[1]),
        ]
        for copy in small:
            copy.start()

    barrier = pltpu.get_barrier_semaphore()
    for k in range(1, shards):
        pl.semaphore_signal(barrier, inc=1, device_id={"shard": lax.rem(me + k, shards)}, device_id_type=MESH)
    if with_router:
        @pl.loop(1, peers)
        def _(k):
            pl.semaphore_signal(barrier, inc=1, device_id={"expert": lax.rem(at + k, peers)}, device_id_type=MESH)
    pl.semaphore_wait(barrier, shards - 1 + (peers - 1 if with_router else 0))

    if with_router:
        mine = pl.ds(pl.multiple_of(me * depth, depth), depth)
        for copy in small:
            copy.wait()
        stage[at, :, mine] = (weight_buf[...] * gain_buf[...]).astype(jnp.bfloat16)

        def hop(k):
            return pltpu.make_async_remote_copy(
                src_ref=stage.at[at, :, mine], dst_ref=stage.at[at, :, mine],
                send_sem=hop_send.at[k - 1], recv_sem=hop_recv.at[k - 1],
                device_id={"expert": lax.rem(at + k, peers)}, device_id_type=MESH,
            )

        def hop_in(k):
            source = lax.rem(at + peers - k, peers)
            return pltpu.make_async_remote_copy(
                src_ref=stage.at[source, :, mine], dst_ref=stage.at[source, :, mine],
                send_sem=hop_send.at[k - 1], recv_sem=hop_recv.at[k - 1],
                device_id={"expert": lax.rem(at + k, peers)}, device_id_type=MESH,
            )

        @pl.loop(1, peers)
        def _(k):
            hop(k).start()

        def rows_to(owner, k):
            columns = pl.ds(pl.multiple_of(owner * depth, depth), depth)
            return pltpu.make_async_remote_copy(
                src_ref=stage.at[:, :, columns], dst_ref=stage.at[:, :, columns],
                send_sem=row_send.at[k - 1], recv_sem=row_recv.at[k - 1],
                device_id={"shard": lax.rem(me + k, shards)}, device_id_type=MESH,
            )

        def pass_on():
            @pl.loop(1, peers)
            def _(k):
                hop(k).wait_send()
                hop_in(k).wait_recv()

            for k in range(1, shards):
                rows_to(me, k).start()

    if experts > 1:
        share_copy.wait()
    shares = share_buf if experts > 1 else mix_ref

    for m, (first, last, sends) in enumerate(plan):
        @pl.loop(0, counts[m])
        def _(i):
            slot = lax.rem(i, SLOTS)
            for copy in load(m, i):
                copy.wait()
            share = shares[first + lax.div(i, per)]
            fresh = share * w_buf[slot] + (1.0 - share) * avg_buf[slot]
            block(m, i, me)[...] = jnp.transpose(fresh.astype(jnp.bfloat16))
            if sends:
                for k in range(1, shards):
                    exchange(m, i, me, k).start()

            if with_router and m == 0:
                pl.when(i == counts[0] // 2)(pass_on)

            @pl.when(i + SLOTS < counts[m])
            def _():
                for copy in load(m, i + SLOTS):
                    copy.start()

            if m + 1 < len(plan):
                @pl.when(i + SLOTS >= counts[m])
                def _():
                    for copy in load(m + 1, i + SLOTS - counts[m]):
                        copy.start()

    if with_router:
        for k in range(1, shards):
            rows_to(me, k).wait_send()
            rows_to(lax.rem(me + shards - k, shards), k).wait_recv()
        held = stage.shape[1]
        for e in range(peers):
            total[e * held:(e + 1) * held, :] = stage[e].astype(jnp.float32)
        router_ref[...] = total[...].astype(jnp.bfloat16)

    for m, (_, _, sends) in enumerate(plan):
        if sends:
            @pl.loop(0, counts[m])
            def _(i):
                for k in range(1, shards):
                    exchange(m, i, me, k).wait_send()
                    exchange(m, i, lax.rem(me + shards - k, shards), k).wait_recv()


def mix(mesh, plan, sources, share, number, router=None):
    peers, shards = mesh.shape["expert"], mesh.shape["shard"]
    experts, depth, width = sources[0].shape
    span = width if BY_COLUMN else depth
    size = min(SIZE, span)
    per = span // size
    assert per % SLOTS == 0
    pieces = sum((last - first) * per for first, last, sends in plan if sends)
    others = max(shards - 1, 1)
    hbm_spec = pl.BlockSpec(memory_space=pltpu.HBM)
    vmem_spec = pl.BlockSpec(memory_space=pltpu.VMEM)
    buffer = pltpu.VMEM((SLOTS, depth, size) if BY_COLUMN else (SLOTS, size, width), jnp.float32)
    out_shape = [
        pltpu.VMEM((last - first, width, (shards if sends else 1) * depth), jnp.bfloat16)
        for first, last, sends in plan
    ]
    share_spec = hbm_spec if experts > 1 else pl.BlockSpec(memory_space=pltpu.SMEM)
    in_specs = [hbm_spec] * len(sources) + [share_spec]
    scratch = [
        buffer,
        buffer,
        pltpu.SMEM(share.shape, jnp.float32),
        pltpu.SemaphoreType.DMA((2, SLOTS)),
        pltpu.SemaphoreType.DMA,
        pltpu.SemaphoreType.DMA((others, pieces)),
        pltpu.SemaphoreType.DMA((others, pieces)),
    ]
    far = functools.partial(pltpu.with_memory_space_constraint, memory_space=pltpu.HBM)
    args = [far(x) for x in sources] + [far(share) if experts > 1 else share]
    if router is not None:
        args += [far(x) for x in router]
        in_specs += [hbm_spec, hbm_spec]
        out_shape += [pltpu.VMEM((peers * experts, shards * depth), jnp.bfloat16)]
        scratch += [
            pltpu.VMEM(router[0].shape, jnp.float32),
            pltpu.VMEM(router[1].shape, jnp.float32),
            pltpu.VMEM((peers, experts, shards * depth), jnp.bfloat16),
            pltpu.VMEM((peers * experts, shards * depth), jnp.float32),
            pltpu.SemaphoreType.DMA((2,)),
            pltpu.SemaphoreType.DMA((peers,)),
            pltpu.SemaphoreType.DMA((peers,)),
            pltpu.SemaphoreType.DMA((others,)),
            pltpu.SemaphoreType.DMA((others,)),
        ]
    moved = sum((last - first) * depth * width * 8 for first, last, _ in plan)
    return pl.pallas_call(
        functools.partial(mix_kernel, peers, shards, size, plan, router is not None),
        out_shape=out_shape,
        in_specs=in_specs,
        out_specs=[vmem_spec] * len(out_shape),
        scratch_shapes=scratch,
        cost_estimate=pl.CostEstimate(flops=0, bytes_accessed=moved, transcendentals=0),
        compiler_params=pltpu.CompilerParams(
            collective_id=number, has_side_effects=True, vmem_limit_bytes=12 * 2**20
        ),
    )(*args)


def store_kernel(place, *refs):
    copies = [
        pltpu.make_async_copy(source, target, refs[-1].at[n])
        for n, (source, target) in enumerate(place(*refs[:-1]))
    ]
    for copy in copies:
        copy.start()
    for copy in copies:
        copy.wait()


def store(place, count, shapes, *arrays):
    vmem_spec = pl.BlockSpec(memory_space=pltpu.VMEM)
    moved = sum(x.size * x.dtype.itemsize for x in arrays)
    return pl.pallas_call(
        functools.partial(store_kernel, place),
        out_shape=[pltpu.HBM(x.shape, x.dtype) for x in shapes],
        in_specs=[vmem_spec] * len(arrays),
        out_specs=[pl.BlockSpec(memory_space=pltpu.HBM)] * len(shapes),
        scratch_shapes=[pltpu.SemaphoreType.DMA((count,))],
        cost_estimate=pl.CostEstimate(flops=0, bytes_accessed=2 * moved, transcendentals=0),
        compiler_params=pltpu.CompilerParams(vmem_limit_bytes=2**20),
    )(*arrays)


def solution(mesh):
    shards = mesh.shape["shard"]

    def local(w_gate, avg_gate, w_up, avg_up, mix_share, router_weight, router_gain):
        experts, depth, width = w_gate.shape
        early = experts // EARLY
        whole = jax.ShapeDtypeStruct((experts, width, shards * depth), jnp.bfloat16)
        plan, sources = [(0, experts, True)], [w_gate, avg_gate]
        if early:
            plan, sources = plan + [(0, early, False)], sources + [w_up, avg_up]
        halves = list(mix(mesh, plan, sources, mix_share, 0))
        held = [
            lax.ppermute(halves[1], "shard", [(n, (n + k) % shards) for n in range(shards)])
            for k in range(1, shards)
        ] if early else []

        def place_gate(gate, gate_out):
            return [(gate.at[e], gate_out.at[e]) for e in range(experts)]

        gate, = store(place_gate, experts, (whole,), halves[0])
        mix_share, gate = lax.optimization_barrier((mix_share, gate))
        late, router = mix(
            mesh, [(early, experts, True)], [w_up, avg_up], mix_share, 1,
            [router_weight.T, router_gain[None, :]],
        )

        def place_up(late, router, *rest):
            *parts, out, router_out = rest
            me = lax.axis_index("shard")
            moves = [(router, router_out)] + [(late.at[e], out.at[early + e]) for e in range(experts - early)]
            for k, part in enumerate(parts):
                owner = lax.rem(me + shards - k, shards)
                column = pl.ds(pl.multiple_of(owner * depth, depth), depth)
                moves += [(part.at[e], out.at[e, :, column]) for e in range(early)]
            return moves

        parts = halves[1:] + held
        count = experts - early + early * len(parts) + 1
        up, router = store(place_up, count, (whole, router), late, router, *parts)
        return gate, up, router.T

    return jax.shard_map(
        local,
        mesh=mesh,
        in_specs=(
            P("expert", "shard", None),
            P("expert", "shard", None),
            P("expert", "shard", None),
            P("expert", "shard", None),
            P("expert"),
            P("shard", "expert"),
            P("shard"),
        ),
        out_specs=(P("expert", None, None), P("expert", None, None), P()),
        check_vma=False,
    )
```

time: 51.7 us -> 45.4 us (0.88)
  local copies, waits for them, and re-layouts: 13.7 us -> 0 us
  Pallas kernels: 37.2 us -> 44 us
  starting transfers between devices: 0 us -> 0.56 us
    unnamed x9 -> x0, local copies, waits for them, and re-layouts: 13.7 us -> none
    pallas_call x2 -> x4, Pallas kernels: 37.2 us -> 44 us  [the longest x2 32.1 us: mix(): pl.pallas_call(functools.partial(mix_kernel, peers, shards, size, plan, r...]
    ppermute x0 -> x1, starting transfers between devices: none -> 0.56 us  [local(): lax.ppermute(halves[1], 'shard', [(n, (n + k) % shards) for n in range(sh...]
  transfers between devices with their start and end apart: 0 -> 1, of which waited for: 0 -> 0; matrix products, arithmetic and copies ran while one was open for 0% -> 0% of each run, Pallas kernels for 0% -> 47%
where the time goes in v3:
time: 45.4 us; the launch traced here: 45.2 us
  Pallas kernels  44 us (97%)
  between operations  0.66 us (1%)
  starting transfers between devices  0.56 us (1%)
    pallas_call x2, Pallas kernels, mix(): pl.pallas_call(functools.partial(mix_kernel, peers, shards, size, plan, r...  32.1 us
    pallas_call x2, Pallas kernels, store(): pl.pallas_call(functools.partial(store_kernel, place), out_shape=[pltpu.H...  12 us
  transfers between devices with their start and end apart: 1, of which 0 were waited for; matrix products, arithmetic and copies ran while one was open for 0% of the time, Pallas kernels for 47%

profile of v3, /device:TPU:0, one launch (start us, length us, event | category | flops | bytes accessed | tf_op | source)
XLA Modules:
  0.0 45.2 jit_solution(4501582103814068448)
XLA Ops:
  0.6 16.6 %shard_map.94 = (bf16[4,1024,2048]{2,1,0:T(8,128)(2,1)S(1)}, bf16[2,1024,1024]{2,1,0:T(8,128)(2,1)S(1)}) custom-call(f32[4,1024,1024]{2,1,0:T(8,128)} %refs_0_.2, f32[4,1024,1024]{2,1,0:T(8,128)} %refs_1_.2, f32[4,1024,1024]{2,1,0:T(8,128)} %refs_0_.3, f32[4,1024,1024]{2,1,0:T(8,128)} %refs_1_.3, f32[4]{0:T(128)} %refs_2_.2), custom_call_target="tpu_custom_call" | custom-call | bytes 50331648 | tf_op jit(solution)/shard_map/pallas_call | solution.py:219
  17.3 0.6 %collective-permute-start = (bf16[2,1024,1024]{2,1,0:T(8,128)(2,1)S(1)}, bf16[2,1024,1024]{2,1,0:T(8,128)(2,1)S(1)}, u32[]{:S(2)}, u32[]{:S(2)}) collective-permute-start(bf16[2,1024,1024]{2,1,0:T(8,128)(2,1)S(1)} %get-tuple-element.16.refs_2_), channel_id=1, source_target_pairs={{0,1},{1,0},{2,3},{3,2},{4,5},{5,4},{6,7},{7,6},{8,9},{9,8},{10,11... | collective-permute-start | bytes 12582920 | tf_op jit(solution)/shard_map/ppermute | solution.py:269
  17.8 5.9 %shard_map.95 = bf16[4,1024,2048]{2,1,0:T(8,128)(2,1)} custom-call(bf16[4,1024,2048]{2,1,0:T(8,128)(2,1)S(1)} %get-tuple-element.11.refs_0_), custom_call_target="tpu_custom_call" | custom-call | bytes 33554432 | tf_op jit(solution)/shard_map/pallas_call | solution.py:246
  23.8 15.4 %shard_map.96 = (bf16[2,1024,2048]{2,1,0:T(8,128)(2,1)S(1)}, bf16[64,2048]{1,0:T(8,128)(2,1)S(1)}) custom-call(f32[4,1024,1024]{2,1,0:T(8,128)} %refs_0_.3, f32[4,1024,1024]{2,1,0:T(8,128)} %refs_1_.3, f32[4]{0:T(128)} %refs_2_.2, f32[4,1024]{1,0:T(4,128)} %bitcast.3, f32[1,1024]{1,0:T(1,128)} %bitcast.4), custom_call_target="tpu_custom_call" | custom-call | bytes 16777216 | tf_op jit(solution)/shard_map/pallas_call | solution.py:219
  39.2 0.0 collective-permute-done.refs_3_
  39.2 6.0 %shard_map.97 = (bf16[4,1024,2048]{2,1,0:T(8,128)(2,1)}, bf16[64,2048]{1,0:T(8,128)(2,1)}) custom-call(bf16[2,1024,2048]{2,1,0:T(8,128)(2,1)S(1)} %get-tuple-element.14.refs_0_, bf16[64,2048]{1,0:T(8,128)(2,1)S(1)} %get-tuple-element.15.refs_1_, bf16[2,1024,1024]{2,1,0:T(8,128)(2,1)S(1)} %get-tuple-element.16.refs_2_, ...), custom_call_target="tpu_custom_call" | custom-call | bytes 34078720 | tf_op jit(solution)/shard_map/pallas_call | solution.py:246
Async XLA Ops:
  17.3 22.0 %collective-permute-start = (bf16[2,1024,1024]{2,1,0:T(8,128)(2,1)S(1)}, bf16[2,1024,1024]{2,1,0:T(8,128)(2,1)S(1)}, u32[]{:S(2)}, u32[]{:S(2)}) collective-permute-start(bf16[2,1024,1024]{2,1,0:T(8,128)(2,1)S(1)} %get-tuple-element.16.refs_2_), channel_id=1, source_target_pairs={{0,1},{1,0},{2,3},{3,2},{4,5},{5,4},{6,7},{7,6},{8,9},{9,8},{10,11... | collective-permute-start | bytes 12582920 | tf_op jit(solution)/shard_map/ppermute | solution.py:269
